TPU v7x, 32 devices: a whole 2x2x4 slice. The times are simulated.
32 devices in a mesh: dp: 8 (over y, x, core), tensor: 4 (over z).
Axes of the slice: x: 2, y: 2, z: 4, core: 2. Of those that a mesh axis runs over, the one named last changes fastest.
Arguments:
- hidden_in: bfloat16 [1024, 2048], P('dp'), may hold values from -6 to 6
- attn_gain: float32 [2048], replicated, may hold values from 0.5 to 1.5
- query_weight: bfloat16 [2048, 2048], P('dp', 'tensor'), may hold values from -0.125 to 0.125
- key_weight: bfloat16 [2048, 2048], P('dp', 'tensor'), may hold values from -0.125 to 0.125
- value_weight: bfloat16 [2048, 2048], P('dp', 'tensor'), may hold values from -0.125 to 0.125
- output_weight: bfloat16 [2048, 2048], P('dp', 'tensor'), may hold values from -1.5 to 1.5
- query_gain: float32 [2048], P('tensor'), may hold values from 0.5 to 1.5
- key_gain: float32 [2048], P('tensor'), may hold values from 0.5 to 1.5
- moe_gain: float32 [2048], replicated, may hold values from 0.5 to 1.5
- expert_gate_up: bfloat16 [2048, 16, 2, 1024], P(None, 'dp', None, 'tensor'), may hold values from -0.125 to 0.125
- expert_down: bfloat16 [2048, 16, 1024], P(None, 'dp', 'tensor'), may hold values from -0.1875 to 0.1875
- experts: int32 [1024, 8], P('dp'), may hold values from 0 to 15, all different within a row
- gates: float32 [1024, 8], P('dp'), may hold values from 0.25 to 0.75
- anchor: int32 [1024], P('dp'), may hold values from 0 to 1023, each once
- lengths: int32 [4], replicated, may hold values from 1 to 512, 1024 in all
- cotangent: bfloat16 [1024, 2048], P('dp'), may hold values from -8 to 8
Outputs:
- output: bfloat16 [1024, 2048], P('dp')
- input_grad: float32 [1024, 2048], P('dp')
- query_grad: float32 [2048, 2048], P('dp', 'tensor')
- key_grad: float32 [2048, 2048], P('dp', 'tensor')
- value_grad: float32 [2048, 2048], P('dp', 'tensor')
- output_grad: float32 [2048, 2048], P('dp', 'tensor')
- gate_up_grad: float32 [2048, 16, 2, 1024], P(None, 'dp', None, 'tensor')
- down_grad: float32 [2048, 16, 1024], P(None, 'dp', 'tensor')
- attn_gain_grad: float32 [2048], P('dp')
- query_gain_grad: float32 [2048], P('dp')
- key_gain_grad: float32 [2048], P('dp')
- moe_gain_grad: float32 [2048], P('dp')
Inputs may be any that keep to these rules, and one draw needn't show every extreme that they name: `anchor`: each number appears once. The lengths sum to 1024; the longest is exactly 512. Each row names 8 different experts.
All inputs are finite; a program needn't handle non-finite values.
Results may differ from a plain program's by a relative error of at most 0.033.
Values may be sent and summed in bfloat16 or wider, within the bound.
A program may use at most 256 MiB of HBM per device.

v0:
```python
import jax
import jax.numpy as jnp
from jax import lax
from jax.sharding import PartitionSpec as P

D = 2048
HD = 128
TOPK = 8
EPSILON = 1e-05
ROPE_BASE = 10000.0
NEG_FILL = -1e30


def rms_norm(values, gain):
    return values * lax.rsqrt(jnp.mean(values * values, axis=-1, keepdims=True) + EPSILON) * gain


def norm_back(values, gain, grad_out):
    inv_rms = lax.rsqrt(jnp.mean(values * values, axis=-1, keepdims=True) + EPSILON)
    weighted = grad_out * gain
    grad_in = inv_rms * weighted - values * inv_rms**3 * jnp.mean(
        weighted * values, axis=-1, keepdims=True
    )
    return (grad_in, jnp.sum(grad_out * values * inv_rms, axis=0))


def locate(anchor, lengths):
    ends = jnp.cumsum(lengths)
    starts = ends - lengths
    docs = jnp.sum((anchor[:, None] >= ends[None, :]).astype(jnp.int32), axis=1)
    which = docs[:, None] == jnp.arange(lengths.shape[0], dtype=jnp.int32)[None, :]
    begins = jnp.sum(jnp.where(which, starts[None, :], 0), axis=1)
    return (docs, (anchor - begins).astype(jnp.int32))


def rotary(tensor, positions):
    half_dim = HD // 2
    freqs = ROPE_BASE ** (-2.0 * jnp.arange(half_dim, dtype=jnp.float32) / HD)
    angles = positions.astype(jnp.float32)[:, None] * freqs[None, :]
    cosine = jnp.cos(angles)[:, None, :]
    sine_part = jnp.sin(angles)[:, None, :]
    first_half = tensor[..., :half_dim]
    second_half = tensor[..., half_dim:]
    return jnp.concatenate(
        [
            first_half * cosine - second_half * sine_part,
            second_half * cosine + first_half * sine_part,
        ],
        axis=-1,
    )


def routing(expert_rows, gate_rows, num_exp, capacity):
    tok_count = expert_rows.shape[0]
    flat_ids = expert_rows.reshape(-1)
    one_hot = (flat_ids[:, None] == jnp.arange(num_exp, dtype=jnp.int32)[None, :]).astype(jnp.int32)
    earlier = jnp.cumsum(one_hot, axis=0) - one_hot
    slot_ids = jnp.sum(earlier * one_hot, axis=1)
    dest_rows = jnp.where(slot_ids < capacity, flat_ids * capacity + slot_ids, num_exp * capacity)
    pair_token = jnp.arange(tok_count * TOPK, dtype=jnp.int32) // TOPK
    slot_source = jnp.zeros((num_exp * capacity + 1,), jnp.int32).at[dest_rows].set(pair_token)
    slot_filled = jnp.zeros((num_exp * capacity + 1,), jnp.float32).at[dest_rows].set(1.0)
    slot_gate = (
        jnp.zeros((num_exp * capacity + 1,), jnp.float32).at[dest_rows].set(gate_rows.reshape(-1))
    )
    return (dest_rows, slot_source[:-1], slot_filled[:-1], slot_gate[:-1])


def pair_allowed(query_anchor, query_docs, key_anchor, key_docs):
    return (
        (query_docs[:, None] == key_docs[None, :]) & (key_anchor[None, :] <= query_anchor[:, None])
    )[None]


def contract_last(left, right):
    return lax.dot_general(
        left, right, (((1,), (1,)), ((), ())), preferred_element_type=jnp.float32
    )


def contract_first(left, right):
    return lax.dot_general(
        left, right, (((0,), (0,)), ((), ())), preferred_element_type=jnp.float32
    )


def shards(
    hidden_in,
    attn_gain,
    query_weight,
    key_weight,
    value_weight,
    output_weight,
    query_gain,
    key_gain,
    moe_gain,
    expert_gate_up,
    expert_down,
    experts,
    gates,
    anchor,
    lengths,
    cotangent,
):
    tok_rows = hidden_in.shape[0]
    head_local = query_weight.shape[1] // HD
    score_scale = HD ** (-0.5)
    f32 = jnp.float32
    bf16 = jnp.bfloat16
    n_dp = lax.axis_size("dp")
    exp_local = expert_down.shape[1]
    num_exp = exp_local * n_dp
    capacity = 9 * tok_rows * TOPK // (8 * num_exp)
    inputs = hidden_in.astype(f32)
    grad_out = cotangent.astype(f32)
    docs, positions = locate(anchor, lengths)
    normed = rms_norm(inputs, attn_gain).astype(bf16)
    query_full, key_full, value_full, output_full = (
        lax.all_gather(query_weight, "dp", axis=0, tiled=True),
        lax.all_gather(key_weight, "dp", axis=0, tiled=True),
        lax.all_gather(value_weight, "dp", axis=0, tiled=True),
        lax.all_gather(output_weight, "dp", axis=0, tiled=True),
    )
    query_raw = jnp.dot(normed, query_full, preferred_element_type=f32)
    key_raw = jnp.dot(normed, key_full, preferred_element_type=f32)
    value_raw = jnp.dot(normed, value_full, preferred_element_type=f32)
    squares = lax.psum(
        (jnp.sum(query_raw * query_raw, axis=1), jnp.sum(key_raw * key_raw, axis=1)), "tensor"
    )
    query_inv = lax.rsqrt(squares[0] / D + EPSILON)[:, None]
    key_inv = lax.rsqrt(squares[1] / D + EPSILON)[:, None]
    query_rows = rotary(
        (query_raw * query_inv * query_gain).reshape(tok_rows, head_local, HD), positions
    ).astype(bf16)
    key_rows = rotary(
        (key_raw * key_inv * key_gain).reshape(tok_rows, head_local, HD), positions
    ).astype(bf16)
    value_rows = value_raw.astype(bf16).reshape(tok_rows, head_local, HD)
    run_max = jnp.full((head_local, tok_rows), NEG_FILL, f32)
    run_acc = jnp.zeros((tok_rows, head_local, HD), f32)
    key_piece = lax.all_gather(key_rows, "dp", axis=0, tiled=True)
    value_piece = lax.all_gather(value_rows, "dp", axis=0, tiled=True)
    anchor_piece = lax.all_gather(anchor, "dp", axis=0, tiled=True)
    piece_docs, unused = locate(anchor_piece, lengths)
    allowed = pair_allowed(anchor, docs, anchor_piece, piece_docs)
    scores = score_scale * jnp.einsum(
        "qhd,khd->hqk", query_rows, key_piece, preferred_element_type=f32
    )
    new_max = jnp.maximum(run_max, jnp.max(jnp.where(allowed, scores, NEG_FILL), axis=2))
    factor = jnp.exp(run_max - new_max)
    attn_probs = jnp.where(allowed, jnp.exp(scores - new_max[:, :, None]), 0.0)
    new_sum = jnp.sum(attn_probs, axis=2)
    update = jnp.einsum(
        "hqk,khd->qhd", attn_probs.astype(bf16), value_piece, preferred_element_type=f32
    )
    run_max, run_sum, run_acc = (new_max, new_sum, run_acc * factor.T[:, :, None] + update)
    log_total = run_max + jnp.log(run_sum)
    attended = run_acc / run_sum.T[:, :, None]
    attended_low = attended.reshape(tok_rows, -1).astype(bf16)
    attn_sum = lax.psum(
        contract_last(attended_low, output_full).astype(jnp.bfloat16), "tensor"
    ).astype(jnp.float32)
    residual = inputs + attn_sum
    moe_in = rms_norm(residual, moe_gain).astype(bf16)
    dest_rows, slot_source, slot_filled, slot_gate = routing(experts, gates, num_exp, capacity)
    buffer_rows = (moe_in[slot_source] * slot_filled[:, None].astype(bf16)).reshape(
        num_exp, capacity, D
    )
    slot_grad = (
        (grad_out[slot_source] * (slot_gate * slot_filled)[:, None])
        .astype(bf16)
        .reshape(num_exp, capacity, D)
    )
    recv_rows, recv_grad = (
        lax.all_to_all(buffer_rows, "dp", split_axis=0, concat_axis=1, tiled=True),
        lax.all_to_all(slot_grad, "dp", split_axis=0, concat_axis=1, tiled=True),
    )
    gate_up = jnp.einsum("ecd,dezf->eczf", recv_rows, expert_gate_up, preferred_element_type=f32)
    gate_part = gate_up[:, :, 0]
    up_part = gate_up[:, :, 1]
    activated = (jax.nn.silu(gate_part) * up_part).astype(bf16)
    expert_out = jnp.einsum("ecf,def->ecd", activated, expert_down, preferred_element_type=f32)
    grad_down = jnp.einsum("ecd,ecf->def", recv_grad, activated, preferred_element_type=f32)
    grad_act = jnp.einsum("ecd,def->ecf", recv_grad, expert_down, preferred_element_type=f32)
    sigmoid_gate = jax.nn.sigmoid(gate_part)
    grad_gate = grad_act * up_part * sigmoid_gate * (1.0 + gate_part * (1.0 - sigmoid_gate))
    grad_up = grad_act * jax.nn.silu(gate_part)
    grad_gateup = jnp.stack([grad_gate, grad_up], axis=2).astype(bf16)
    grad_gateup_w = jnp.einsum("ecd,eczf->dezf", recv_rows, grad_gateup, preferred_element_type=f32)
    grad_buffer = jnp.einsum(
        "eczf,dezf->ecd", grad_gateup, expert_gate_up, preferred_element_type=f32
    )
    back_out, back_grad = (
        lax.all_to_all(
            expert_out.astype(jnp.bfloat16), "dp", split_axis=1, concat_axis=0, tiled=True
        ).astype(expert_out.dtype),
        lax.all_to_all(
            grad_buffer.astype(jnp.bfloat16), "dp", split_axis=1, concat_axis=0, tiled=True
        ).astype(grad_buffer.dtype),
    )
    width = back_out.shape[2]
    zero_row = jnp.zeros((1, width), f32)
    table_rows = jnp.concatenate([back_out.reshape(num_exp * capacity, width), zero_row], axis=0)
    combined = jnp.sum(
        table_rows[dest_rows].reshape(tok_rows, TOPK, width) * gates[:, :, None], axis=1
    )
    grad_table = jnp.concatenate([back_grad.reshape(num_exp * capacity, width), zero_row], axis=0)
    grad_moe_part = jnp.sum(grad_table[dest_rows].reshape(tok_rows, TOPK, width), axis=1)
    moe_sum, grad_moe_in = (
        lax.psum(combined.astype(jnp.bfloat16), "tensor").astype(jnp.float32),
        lax.psum(grad_moe_part.astype(jnp.bfloat16), "tensor").astype(jnp.float32),
    )
    output = (residual + moe_sum).astype(bf16)
    query_full, key_full, value_full, output_full = (
        lax.all_gather(query_weight, "dp", axis=0, tiled=True),
        lax.all_gather(key_weight, "dp", axis=0, tiled=True),
        lax.all_gather(value_weight, "dp", axis=0, tiled=True),
        lax.all_gather(output_weight, "dp", axis=0, tiled=True),
    )
    grad_norm_moe, grad_moe_gain = norm_back(residual, moe_gain, grad_moe_in)
    grad_resid = grad_out + grad_norm_moe
    grad_resid_low = grad_resid.astype(bf16)
    grad_output_w = contract_first(grad_resid_low, attended_low)
    grad_att_low = (
        jnp.dot(grad_resid_low, output_full, preferred_element_type=f32)
        .astype(bf16)
        .reshape(tok_rows, head_local, HD)
    )
    delta_rows = jnp.sum(grad_att_low.astype(f32) * attended, axis=2).T
    key_piece = lax.all_gather(key_rows, "dp", axis=0, tiled=True)
    value_piece = lax.all_gather(value_rows, "dp", axis=0, tiled=True)
    anchor_piece = lax.all_gather(anchor, "dp", axis=0, tiled=True)
    piece_docs, unused = locate(anchor_piece, lengths)
    allowed = pair_allowed(anchor, docs, anchor_piece, piece_docs)
    scores = score_scale * jnp.einsum(
        "qhd,khd->hqk", query_rows, key_piece, preferred_element_type=f32
    )
    attn_probs = jnp.where(allowed, jnp.exp(scores - log_total[:, :, None]), 0.0)
    grad_probs = jnp.einsum("qhd,khd->hqk", grad_att_low, value_piece, preferred_element_type=f32)
    grad_scores = (attn_probs * (grad_probs - delta_rows[:, :, None])).astype(bf16)
    grad_query_rot = score_scale * jnp.einsum(
        "hqk,khd->qhd", grad_scores, key_piece, preferred_element_type=f32
    )
    query_wide = lax.all_gather(
        query_rows.astype(f32).astype(jnp.bfloat16), "dp", axis=0, tiled=True
    ).astype(jnp.float32)
    gradatt_wide = lax.all_gather(
        grad_att_low.astype(f32).astype(jnp.bfloat16), "dp", axis=0, tiled=True
    ).astype(jnp.float32)
    logtot_piece = lax.all_gather(
        log_total.T.astype(jnp.bfloat16), "dp", axis=0, tiled=True
    ).astype(jnp.float32)
    delta_piece = lax.all_gather(
        delta_rows.T.astype(jnp.bfloat16), "dp", axis=0, tiled=True
    ).astype(jnp.float32)
    anchor_piece = lax.all_gather(anchor, "dp", axis=0, tiled=True)
    query_piece = query_wide.astype(bf16)
    gradatt_piece = gradatt_wide.astype(bf16)
    piece_docs, unused = locate(anchor_piece, lengths)
    allowed = pair_allowed(anchor_piece, piece_docs, anchor, docs)
    scores = score_scale * jnp.einsum(
        "qhd,khd->hqk", query_piece, key_rows, preferred_element_type=f32
    )
    attn_probs = jnp.where(allowed, jnp.exp(scores - logtot_piece.T[:, :, None]), 0.0)
    grad_value = jnp.einsum(
        "hqk,qhd->khd", attn_probs.astype(bf16), gradatt_piece, preferred_element_type=f32
    )
    grad_probs = jnp.einsum("qhd,khd->hqk", gradatt_piece, value_rows, preferred_element_type=f32)
    grad_scores = (attn_probs * (grad_probs - delta_piece.T[:, :, None])).astype(bf16)
    grad_key = score_scale * jnp.einsum(
        "hqk,qhd->khd", grad_scores, query_piece, preferred_element_type=f32
    )
    grad_query_hat = rotary(grad_query_rot, -positions).reshape(tok_rows, -1)
    grad_key_hat = rotary(grad_key, -positions).reshape(tok_rows, -1)
    weighted_query = grad_query_hat * query_gain
    weighted_key = grad_key_hat * key_gain
    quarter = query_gain.shape[0]
    gain_offset = lax.axis_index("tensor") * quarter
    query_gain_part = jnp.sum(grad_query_hat * query_raw * query_inv, axis=0)
    key_gain_part = jnp.sum(grad_key_hat * key_raw * key_inv, axis=0)
    query_gain_wide = lax.dynamic_update_slice_in_dim(
        jnp.zeros((D,), f32), query_gain_part, gain_offset, 0
    )
    key_gain_wide = lax.dynamic_update_slice_in_dim(
        jnp.zeros((D,), f32), key_gain_part, gain_offset, 0
    )
    cross = lax.psum(
        (
            jnp.sum(weighted_query * query_raw, axis=1),
            jnp.sum(weighted_key * key_raw, axis=1),
            query_gain_wide,
            key_gain_wide,
        ),
        "tensor",
    )
    grad_query_raw = (
        query_inv * weighted_query - query_raw * query_inv**3 * cross[0][:, None] / D
    ).astype(bf16)
    grad_key_raw = (key_inv * weighted_key - key_raw * key_inv**3 * cross[1][:, None] / D).astype(
        bf16
    )
    grad_value_low = grad_value.reshape(tok_rows, -1).astype(bf16)
    grad_query_w = contract_first(normed, grad_query_raw)
    grad_key_w = contract_first(normed, grad_key_raw)
    grad_value_w = contract_first(normed, grad_value_low)
    grad_normed = (
        contract_last(grad_query_raw, query_full)
        + contract_last(grad_key_raw, key_full)
        + contract_last(grad_value_low, value_full)
    )
    grad_normed_sum = lax.psum(grad_normed.astype(jnp.bfloat16), "tensor").astype(jnp.float32)
    grad_norm_attn, grad_attn_gain = norm_back(inputs, attn_gain, grad_normed_sum)
    input_grad = grad_resid + grad_norm_attn
    summed = (
        lax.psum_scatter(
            grad_query_w.astype(jnp.bfloat16), "dp", scatter_dimension=0, tiled=True
        ).astype(jnp.float32),
        lax.psum_scatter(
            grad_key_w.astype(jnp.bfloat16), "dp", scatter_dimension=0, tiled=True
        ).astype(jnp.float32),
        lax.psum_scatter(
            grad_value_w.astype(jnp.bfloat16), "dp", scatter_dimension=0, tiled=True
        ).astype(jnp.float32),
        lax.psum_scatter(
            grad_output_w.astype(jnp.bfloat16), "dp", scatter_dimension=0, tiled=True
        ).astype(jnp.float32),
        lax.psum_scatter(
            grad_attn_gain.astype(jnp.bfloat16), "dp", scatter_dimension=0, tiled=True
        ).astype(jnp.float32),
        lax.psum_scatter(
            cross[2].astype(jnp.bfloat16), "dp", scatter_dimension=0, tiled=True
        ).astype(jnp.float32),
        lax.psum_scatter(
            cross[3].astype(jnp.bfloat16), "dp", scatter_dimension=0, tiled=True
        ).astype(jnp.float32),
        lax.psum_scatter(
            grad_moe_gain.astype(jnp.bfloat16), "dp", scatter_dimension=0, tiled=True
        ).astype(jnp.float32),
    )
    return (
        output,
        input_grad,
        summed[0],
        summed[1],
        summed[2],
        summed[3],
        grad_gateup_w,
        grad_down,
        summed[4],
        summed[5],
        summed[6],
        summed[7],
    )


def solution(mesh):
    in_specs = (
        P("dp", None),
        P(),
        P("dp", "tensor"),
        P("dp", "tensor"),
        P("dp", "tensor"),
        P("dp", "tensor"),
        P("tensor"),
        P("tensor"),
        P(),
        P(None, "dp", None, "tensor"),
        P(None, "dp", "tensor"),
        P("dp", None),
        P("dp", None),
        P("dp"),
        P(),
        P("dp", None),
    )
    out_specs = (
        P("dp", None),
        P("dp", None),
        P("dp", "tensor"),
        P("dp", "tensor"),
        P("dp", "tensor"),
        P("dp", "tensor"),
        P(None, "dp", None, "tensor"),
        P(None, "dp", "tensor"),
        P("dp"),
        P("dp"),
        P("dp"),
        P("dp"),
    )
    return jax.shard_map(shards, mesh=mesh, in_specs=in_specs, out_specs=out_specs, check_vma=False)
```

profile of v0, /device:TPU:0, one launch (start us, length us, event | category | flops | bytes accessed | tf_op | source)
XLA Modules:
  0.0 867.9 jit_solution(12070746928078635573)
XLA Ops:
  15.4 25.0 %all-gather.10.cloned.1.call-done = bf16[2048,512]{1,0:T(8,128)(2,1)} async-done(((bf16[256,512]{1,0:T(8,128)(2,1)}), bf16[2048,512]{1,0:T(8,128)(2,1)}) %all-gather.10.cloned.1.call-update) | async-done | bytes 2097168 | tf_op jit(solution)/shard_map/all_gather | solution.py:119
  42.8 27.3 %all-gather.12.cloned.1.call-done = bf16[2048,512]{1,0:T(8,128)(2,1)} async-done(((bf16[256,512]{1,0:T(8,128)(2,1)}), bf16[2048,512]{1,0:T(8,128)(2,1)}) %all-gather.12.cloned.1.call-update) | async-done | bytes 2097168 | tf_op jit(solution)/shard_map/all_gather | solution.py:120
  72.3 11.7 %all-reduce.7 = (f32[128]{0:T(128)S(1)}, f32[128]{0:T(128)S(1)}) all-reduce(f32[128]{0:T(128)S(1)} %get-tuple-element.131, f32[128]{0:T(128)S(1)} %get-tuple-element.133), channel_id=1, replica_groups=mesh['dp'=8,'tensor'=4] {'tensor'}, use_global_device_ids=true, to_apply=%region_5.6 | all-reduce | flops 256 | bytes 2048 | tf_op jit(solution)/shard_map/psum | solution.py:127
  141.4 65.4 %all-gather = s32[8,1,128]{2,1,0:T(1,128)S(1)} all-gather(s32[1,1,128]{2,1,0:T(1,128)S(1)} %bitcast.187), channel_id=1, replica_groups=mesh['dp'=8,'tensor'=4] {'dp'}, dimensions={0}, use_global_device_ids=true | all-gather | bytes 4608 | tf_op jit(solution)/shard_map/all_gather | solution.py:143
  218.9 38.4 %all-reduce.14.cloned.1.call-done = bf16[128,2048]{1,0:T(8,128)(2,1)} async-done(((bf16[128,2048]{1,0:T(8,128)(2,1)}), bf16[128,2048]{1,0:T(8,128)(2,1)}) %all-reduce.14.cloned.1.call-update) | async-done | bytes 524304 | tf_op jit(solution)/shard_map/psum | solution.py:160
  281.0 49.4 %all-to-all-done = bf16[16,72,2048]{2,1,0:T(8,128)(2,1)} async-done(((bf16[16,72,2048]{2,1,0:T(8,128)(2,1)}), bf16[16,72,2048]{2,1,0:T(8,128)(2,1)}, u32[]{:S(2)}, u32[]{:S(2)}) %all-to-all-start) | async-done | bytes 4718624 | tf_op jit(solution)/shard_map/all_to_all | solution.py:175
  344.5 9.4 %copy.183 = bf16[2,576,2048]{2,0,1:T(2,128)(2,1)} copy(bf16[2,576,2048]{2,1,0:T(8,128)(2,1)} %bitcast_convert_fusion) | data formatting | bytes 9437184 | tf_op jit(solution)/shard_map/convert_element_type | solution.py:198
  362.5 9.3 %copy.176 = bf16[2,576,2048]{2,0,1:T(2,128)(2,1)} copy(bf16[2,576,2048]{2,1,0:T(8,128)(2,1)} %convolution_convert_fusion) | data formatting | bytes 9437184 | tf_op jit(solution)/shard_map/convert_element_type | solution.py:195
  371.8 41.7 %all-to-all-done.3 = bf16[2,576,2048]{2,0,1:T(2,128)(2,1)} async-done(((bf16[2,576,2048]{2,0,1:T(2,128)(2,1)}), bf16[2,576,2048]{2,0,1:T(2,128)(2,1)}, u32[]{:S(2)}, u32[]{:S(2)}) %all-to-all-start.3) | async-done | bytes 4718624 | tf_op jit(solution)/shard_map/all_to_all | solution.py:197
  419.4 60.7 %all_gather.49 = bf16[1024,4]{0,1:T(4,128)(2,1)S(1)} all-gather(bf16[128,4]{0,1:T(4,128)(2,1)S(1)} %copy-done.64), channel_id=1, replica_groups=mesh['dp'=8,'tensor'=4] {'dp'}, dimensions={0}, use_global_device_ids=true | all-gather | bytes 9216 | tf_op jit(solution)/shard_map/all_gather | solution.py:250
  489.5 12.6 %gather_fusion.3 = f32[1024,2048]{1,0:T(8,128)} fusion(f32[1153,2048]{1,0:T(8,128)} %pad_convert_fusion, s32[1024]{0:T(1024)S(1)} %broadcast_clamp_fusion), kind=kCustom, calls=%fused_computation.3 | custom fusion | bytes 16781312 | tf_op jit(solution)/shard_map/gather | solution.py:208
  518.5 26.7 %all-reduce.16.cloned.1.call-done = bf16[128,2048]{1,0:T(8,128)(2,1)} async-done(((bf16[128,2048]{1,0:T(8,128)(2,1)}), bf16[128,2048]{1,0:T(8,128)(2,1)}) %all-reduce.16.cloned.1.call-update) | async-done | bytes 524304 | tf_op jit(solution)/shard_map/psum | solution.py:211
  550.7 7.3 pad_convert_fusion.1
  557.9 12.6 %gather_fusion.1 = f32[1024,2048]{1,0:T(8,128)} fusion(f32[1153,2048]{1,0:T(8,128)} %pad_convert_fusion.1, s32[1024]{0:T(1024)S(1)} %broadcast_clamp_fusion), kind=kCustom, calls=%fused_computation.1 | custom fusion | bytes 16781312 | tf_op jit(solution)/shard_map/gather | solution.py:205
  570.5 7.5 fusion
  578.1 8.9 %all_gather.51 = bf16[1024,4]{0,1:T(4,128)(2,1)S(1)} all-gather(bf16[128,4]{0,1:T(4,128)(2,1)S(1)} %convert_element_type.256), channel_id=1, replica_groups=mesh['dp'=8,'tensor'=4] {'dp'}, dimensions={0}, use_global_device_ids=true | all-gather | bytes 9216 | tf_op jit(solution)/shard_map/all_gather | solution.py:253
  605.2 19.0 %all-reduce.6 = (f32[128]{0:T(128)}, f32[128]{0:T(128)S(1)}, bf16[2048]{0:T(1024)(128)(2,1)}, bf16[2048]{0:T(1024)(128)(2,1)}) all-reduce(f32[128]{0:T(128)S(1)} %get-tuple-element.79, f32[128]{0:T(128)} %get-tuple-element.77, f32[2048]{0:T(1024)S(1)} %dynamic_update_slice.6, ...), channel_id=1, replica_groups=mesh['dp'=8,'tensor'=4] {'tensor'}, use_global_device_ids=true, to_apply=%region_26.27 | all-reduce | flops 4352 | bytes 26624 | tf_op jit(solution)/shard_map/psum | solution.py:287
  645.2 8.2 convolution_bitcast_fusion
  653.4 13.3 %copy.195 = f32[2048,2,2,256]{3,2,1,0:T(2,128)} copy(f32[2048,2,2,256]{0,3,2,1:T(8,128)} %convolution_bitcast_fusion) | data formatting | bytes 16777216
  684.0 24.2 %all-reduce.8 = (bf16[2048]{0:T(1024)(128)(2,1)S(1)}, bf16[2048]{0:T(1024)(128)(2,1)S(1)}, bf16[2048]{0:T(1024)(128)(2,1)S(1)}, bf16[2048]{0:T(1024)(128)(2,1)S(1)}) all-reduce(bf16[2048]{0:T(1024)(128)(2,1)S(1)} %get-tuple-element.74, bf16[2048]{0:T(1024)(128)(2,1)S(1)} %copy-done.65, ...), channel_id=6, replica_groups=mesh['dp'=8,'tensor'=4] {'dp'}, use_global_device_ids=true, to_apply=%region_36.37.clone | all-reduce | flops 8192 | bytes 32768
  714.5 11.6 %reduce-scatter.11.cloned.1.call-done = bf16[256,512]{1,0:T(8,128)(2,1)} async-done(((bf16[2048,512]{1,0:T(8,128)(2,1)}), bf16[256,512]{1,0:T(8,128)(2,1)}) %reduce-scatter.11.cloned.1.call-update) | async-done | bytes 262160 | tf_op jit(solution)/shard_map/reduce_scatter | solution.py:324
  727.9 42.6 %reduce-scatter.9.cloned.1.call-done = bf16[256,512]{1,0:T(8,128)(2,1)} async-done(((bf16[2048,512]{1,0:T(8,128)(2,1)}), bf16[256,512]{1,0:T(8,128)(2,1)}) %reduce-scatter.9.cloned.1.call-update) | async-done | bytes 262160 | tf_op jit(solution)/shard_map/reduce_scatter | solution.py:321
  772.4 42.5 %reduce-scatter.7.cloned.1.call-done = bf16[256,512]{1,0:T(8,128)(2,1)} async-done(((bf16[2048,512]{1,0:T(8,128)(2,1)}), bf16[256,512]{1,0:T(8,128)(2,1)}) %reduce-scatter.7.cloned.1.call-update) | async-done | bytes 262160 | tf_op jit(solution)/shard_map/reduce_scatter | solution.py:318
  816.7 42.5 %reduce-scatter.5.cloned.1.call-done = bf16[256,512]{1,0:T(8,128)(2,1)} async-done(((bf16[2048,512]{1,0:T(8,128)(2,1)}), bf16[256,512]{1,0:T(8,128)(2,1)}) %reduce-scatter.5.cloned.1.call-update) | async-done | bytes 262160 | tf_op jit(solution)/shard_map/reduce_scatter | solution.py:315
  (345 shorter events, 233.9 us)
Async XLA Ops:
  7.2 329.5 %copy-start = (bf16[2048,2,256]{2,1,0:T(2,128)(2,1)S(1)}, bf16[2048,2,256]{2,1,0:T(2,128)(2,1)}, u32[]{:S(2)}) copy-start(bf16[2048,2,256]{2,1,0:T(2,128)(2,1)} %param.26) | copy-start | bytes 6291460
  7.2 33.2 %all-gather.10.cloned.1.call-start = ((), (), s32[]{:S(2)}) async-start(), calls=%async_computation.8 | async-start | bytes 2359296 | tf_op jit(solution)/shard_map/all_gather | solution.py:119
  7.9 62.2 %all-gather.12.cloned.1.call-start = ((), (), s32[]{:S(2)}) async-start(), calls=%async_computation.9 | async-start | bytes 2359296 | tf_op jit(solution)/shard_map/all_gather | solution.py:120
  8.7 91.1 %all-gather.16.cloned.1.call-start = ((), (), s32[]{:S(2)}) async-start(), calls=%async_computation.11 | async-start | bytes 2359296 | tf_op jit(solution)/shard_map/all_gather | solution.py:121
  9.4 198.1 %all-gather.14.cloned.1.call-start = ((), (), s32[]{:S(2)}) async-start(), calls=%async_computation.10 | async-start | bytes 1179648 | tf_op jit(solution)/shard_map/all_gather | solution.py:141
  15.4 84.4 %copy-start.53 = (f32[128]{0:T(128)}, f32[128]{0:T(128)S(1)}, u32[]{:S(2)}) copy-start(f32[128]{0:T(128)S(1)} %get-tuple-element.122) | copy-start | bytes 1540
  93.2 118.8 %all-gather.18.cloned.1.call-start = ((), (), s32[]{:S(2)}) async-start(), calls=%async_computation.12 | async-start | bytes 1179648 | tf_op jit(solution)/shard_map/all_gather | solution.py:142
  102.7 112.7 %all-gather.20.cloned.1.call-start = ((), (), s32[]{:S(2)}) async-start(), calls=%async_computation.13 | async-start | bytes 2359296 | tf_op jit(solution)/shard_map/all_gather | solution.py:122
  136.5 70.9 %copy-start.26 = (bf16[128,4,64]{2,0,1:T(8,128)(2,1)S(1)}, bf16[128,4,64]{2,0,1:T(8,128)(2,1)}, u32[]{:S(2)}) copy-start(bf16[128,4,64]{2,0,1:T(8,128)(2,1)} %get-tuple-element.109) | copy-start | bytes 196612
  136.5 70.9 %copy-start.27 = (bf16[128,4,64]{2,0,1:T(8,128)(2,1)S(1)}, bf16[128,4,64]{2,0,1:T(8,128)(2,1)}, u32[]{:S(2)}) copy-start(bf16[128,4,64]{2,0,1:T(8,128)(2,1)} %get-tuple-element.110) | copy-start | bytes 196612
  136.6 134.6 %all-to-all-start.2 = ((bf16[16,72,2048]{2,1,0:T(8,128)(2,1)}), bf16[16,72,2048]{2,1,0:T(8,128)(2,1)}, u32[]{:S(2)}, u32[]{:S(2)}) async-start(bf16[16,72,2048]{2,1,0:T(8,128)(2,1)} %multiply_convert_fusion), calls=%async_computation.2 | async-start | bytes 9437184 | tf_op jit(solution)/shard_map/all_to_all | solution.py:176
  141.3 115.9 %all-reduce.14.cloned.1.call-start = ((), (), s32[]{:S(2)}) async-start(), calls=%async_computation.14 | async-start | bytes 1048576 | tf_op jit(solution)/shard_map/psum | solution.py:160
  271.2 59.3 %all-to-all-start = ((bf16[16,72,2048]{2,1,0:T(8,128)(2,1)}), bf16[16,72,2048]{2,1,0:T(8,128)(2,1)}, u32[]{:S(2)}, u32[]{:S(2)}) async-start(bf16[16,72,2048]{2,1,0:T(8,128)(2,1)} %broadcast_multiply_fusion), calls=%async_computation | async-start | bytes 9437184 | tf_op jit(solution)/shard_map/all_to_all | solution.py:175
  353.8 59.8 %all-to-all-start.3 = ((bf16[2,576,2048]{2,0,1:T(2,128)(2,1)}), bf16[2,576,2048]{2,0,1:T(2,128)(2,1)}, u32[]{:S(2)}, u32[]{:S(2)}) async-start(bf16[2,576,2048]{2,0,1:T(2,128)(2,1)} %copy.183), calls=%async_computation.3 | async-start | bytes 9437184 | tf_op jit(solution)/shard_map/all_to_all | solution.py:197
  413.6 98.2 %all-to-all-start.1 = ((bf16[2,576,2048]{2,0,1:T(2,128)(2,1)}), bf16[2,576,2048]{2,0,1:T(2,128)(2,1)}, u32[]{:S(2)}, u32[]{:S(2)}) async-start(bf16[2,576,2048]{2,0,1:T(2,128)(2,1)} %copy.176), calls=%async_computation.1 | async-start | bytes 9437184 | tf_op jit(solution)/shard_map/all_to_all | solution.py:194
  418.2 90.2 %all-gather.22.cloned.1.call-start = ((), (), s32[]{:S(2)}) async-start(), calls=%async_computation.16 | async-start | bytes 1179648 | tf_op jit(solution)/shard_map/all_gather | solution.py:244
  419.0 126.2 %all-reduce.16.cloned.1.call-start = ((), (), s32[]{:S(2)}) async-start(), calls=%async_computation.15 | async-start | bytes 1048576 | tf_op jit(solution)/shard_map/psum | solution.py:211
  508.3 82.3 %all-gather.24.cloned.1.call-start = ((), (), s32[]{:S(2)}) async-start(), calls=%async_computation.17 | async-start | bytes 1179648 | tf_op jit(solution)/shard_map/all_gather | solution.py:247
  550.4 132.2 %all-reduce.18.cloned.1.call-start = ((), (), s32[]{:S(2)}) async-start(), calls=%async_computation.22 | async-start | bytes 2097152 | tf_op jit(solution)/shard_map/psum | solution.py:210
  633.2 92.9 %reduce-scatter.11.cloned.1.call-start = ((), (), s32[]{:S(2)}) async-start(), calls=%async_computation.21 | async-start | bytes 2359296 | tf_op jit(solution)/shard_map/reduce_scatter | solution.py:324
  636.5 134.1 %reduce-scatter.9.cloned.1.call-start = ((), (), s32[]{:S(2)}) async-start(), calls=%async_computation.20 | async-start | bytes 2359296 | tf_op jit(solution)/shard_map/reduce_scatter | solution.py:321
  639.4 175.5 %reduce-scatter.7.cloned.1.call-start = ((), (), s32[]{:S(2)}) async-start(), calls=%async_computation.19 | async-start | bytes 2359296 | tf_op jit(solution)/shard_map/reduce_scatter | solution.py:318
  641.7 217.5 %reduce-scatter.5.cloned.1.call-start = ((), (), s32[]{:S(2)}) async-start(), calls=%async_computation.18 | async-start | bytes 2359296 | tf_op jit(solution)/shard_map/reduce_scatter | solution.py:315
  710.8 150.1 %copy-start.1 = (bf16[2048,2,256]{2,1,0:T(2,128)(2,1)S(1)}, bf16[2048,2,256]{2,1,0:T(2,128)(2,1)}, u32[]{:S(2)}) copy-start(bf16[2048,2,256]{2,1,0:T(2,128)(2,1)} %param.26) | copy-start | bytes 6291460
  (81 other events, 1464.9 us)
Sparse Core Ops, SparseCore 0:
  9.9 30.4 all-gather.9
  42.3 27.7 all-gather.11
  72.0 27.7 all-gather.15
  102.2 23.3 all-gather.13
  127.9 26.3 all-gather.17
  156.0 52.6 all-gather.19
  218.9 38.3 all-reduce.13
  420.9 35.1 all-gather.21
  508.5 36.7 all-reduce.15
  550.5 23.2 all-gather.23
  633.3 49.2 all-reduce.17
  685.8 40.3 reduce-scatter.10
  729.4 41.1 reduce-scatter.8
  773.7 41.1 reduce-scatter.6
  818.0 41.1 reduce-scatter.4
where the time goes:
time: 877 us; the launch traced here: 868 us
  waiting for transfers between devices  360 us (41%)
  blocking collectives  190 us (22%)
  local copies, waits for them, and re-layouts  129 us (15%)
  other arithmetic  83.5 us (10%)
  matrix products  69.1 us (8%)
  starting transfers between devices  20.1 us (2%)
  between operations  16.2 us (2%)
    all_gather x1, blocking collectives, shards(): anchor_piece = lax.all_gather(anchor, 'dp', axis=0, tiled=True)  65.4 us
    all_gather x1, blocking collectives, shards(): lax.all_gather(log_total.T.astype(jnp.bfloat16), 'dp', axis=0, tiled=True)  60.7 us
    all_to_all x1, waiting for transfers between devices, shards(): lax.all_to_all(buffer_rows, 'dp', split_axis=0, concat_axis=1, tiled=True)  49.4 us
    reduce_scatter x1, waiting for transfers between devices, shards(): lax.psum_scatter(grad_value_w.astype(jnp.bfloat16), 'dp', scatter_dimensi...  42.6 us
    reduce_scatter x1, waiting for transfers between devices, shards(): lax.psum_scatter(grad_key_w.astype(jnp.bfloat16), 'dp', scatter_dimension...  42.5 us
    reduce_scatter x1, waiting for transfers between devices, shards(): lax.psum_scatter(grad_query_w.astype(jnp.bfloat16), 'dp', scatter_dimensi...  42.5 us
    all_to_all x1, waiting for transfers between devices, shards(): lax.all_to_all(grad_buffer.astype(jnp.bfloat16), 'dp', split_axis=1, conc...  41.7 us
    psum x1, waiting for transfers between devices, shards(): lax.psum(contract_last(attended_low, output_full).astype(jnp.bfloat16), '...  38.4 us
  transfers between devices with their start and end apart: 19, of which 12 were waited for; matrix products, arithmetic and copies ran while one was open for 26% of the time, Pallas kernels for 0%

commit v1 on v0

--- a/solution.py
+++ b/solution.py
@@ -9,6 +9,19 @@
 EPSILON = 1e-05
 ROPE_BASE = 10000.0
 NEG_FILL = -1e30
+
+
+def ring_gather(shard, axis, dim):
+    ways = lax.axis_size(axis)
+    up = [(d, (d + 1) % ways) for d in range(ways)]
+    down = [(d, (d - 1) % ways) for d in range(ways)]
+    earlier, later = ([shard], [shard])
+    for _ in range(ways // 2):
+        earlier.append(lax.ppermute(earlier[-1], axis, up))
+    for _ in range((ways - 1) // 2):
+        later.append(lax.ppermute(later[-1], axis, down))
+    line = jnp.concatenate([*earlier[::-1], *later[1:]], axis=dim)
+    return jnp.roll(line, (lax.axis_index(axis) - ways // 2) * shard.shape[dim], axis=dim)
 
 
 def rms_norm(values, gain):
@@ -117,7 +130,7 @@
     normed = rms_norm(inputs, attn_gain).astype(bf16)
     query_full, key_full, value_full, output_full = (
         lax.all_gather(query_weight, "dp", axis=0, tiled=True),
-        lax.all_gather(key_weight, "dp", axis=0, tiled=True),
+        ring_gather(key_weight, "dp", 0),
         lax.all_gather(value_weight, "dp", axis=0, tiled=True),
         lax.all_gather(output_weight, "dp", axis=0, tiled=True),
     )

time: 877 us -> 837 us (0.954)
  waiting for transfers between devices: 360 us -> 311 us
  blocking collectives: 190 us -> 173 us
  starting transfers between devices: 20.1 us -> 32.9 us
  matrix products: 69.1 us -> 78.7 us
    all_gather x1, waiting for transfers between devices: 27.3 us -> 0.01 us  [shards(): lax.all_gather(key_weight, 'dp', axis=0, tiled=True)]
    all_gather x1, waiting for transfers between devices: 25 us -> 0.02 us  [shards(): lax.all_gather(query_weight, 'dp', axis=0, tiled=True)]
    all_gather x1, blocking collectives: 60.7 us -> 36.2 us  [shards(): lax.all_gather(log_total.T.astype(jnp.bfloat16), 'dp', axis=0, tiled=True)]
    ppermute x0 -> x7, waiting for transfers between devices: none -> 13.2 us  [the longest x4 13.2 us: ring_gather(): earlier.append(lax.ppermute(earlier[-1], axis, up))]
    all_to_all x1, waiting for transfers between devices: 41.7 us -> 54.2 us  [shards(): lax.all_to_all(grad_buffer.astype(jnp.bfloat16), 'dp', split_axis=1, conc...]
    ppermute x0 -> x7, starting transfers between devices: none -> 12 us  [the longest x4 8.91 us: ring_gather(): earlier.append(lax.ppermute(earlier[-1], axis, up))]
    psum x1, waiting for transfers between devices: 26.7 us -> 17.1 us  [shards(): lax.psum(grad_moe_part.astype(jnp.bfloat16), 'tensor').astype(jnp.float32)]
    unnamed x177 -> x134, local copies, waits for them, and re-layouts: 28.1 us -> 33.4 us
  transfers between devices with their start and end apart: 19 -> 26, of which waited for: 12 -> 12; matrix products, arithmetic and copies ran while one was open for 26% -> 28% of each run, Pallas kernels for 0% -> 0%
where the time goes in v1:
time: 837 us; the launch traced here: 827 us
  waiting for transfers between devices  311 us (37%)
  blocking collectives  173 us (21%)
  local copies, waits for them, and re-layouts  132 us (16%)
  other arithmetic  82.3 us (10%)
  matrix products  78.7 us (9%)
  starting transfers between devices  32.9 us (4%)
  between operations  16.1 us (2%)
    all_gather x1, blocking collectives, shards(): anchor_piece = lax.all_gather(anchor, 'dp', axis=0, tiled=True)  67.7 us
    all_to_all x1, waiting for transfers between devices, shards(): lax.all_to_all(grad_buffer.astype(jnp.bfloat16), 'dp', split_axis=1, conc...  54.2 us
    all_to_all x1, waiting for transfers between devices, shards(): lax.all_to_all(buffer_rows, 'dp', split_axis=0, concat_axis=1, tiled=True)  49.4 us
    reduce_scatter x1, waiting for transfers between devices, shards(): lax.psum_scatter(grad_value_w.astype(jnp.bfloat16), 'dp', scatter_dimensi...  42.6 us
    reduce_scatter x1, waiting for transfers between devices, shards(): lax.psum_scatter(grad_query_w.astype(jnp.bfloat16), 'dp', scatter_dimensi...  42.5 us
    reduce_scatter x1, waiting for transfers between devices, shards(): lax.psum_scatter(grad_key_w.astype(jnp.bfloat16), 'dp', scatter_dimension...  42.5 us
    all_gather x1, blocking collectives, shards(): lax.all_gather(log_total.T.astype(jnp.bfloat16), 'dp', axis=0, tiled=True)  36.2 us
    psum x1, waiting for transfers between devices, shards(): lax.psum(contract_last(attended_low, output_full).astype(jnp.bfloat16), '...  35.5 us
  transfers between devices with their start and end apart: 26, of which 12 were waited for; matrix products, arithmetic and copies ran while one was open for 28% of the time, Pallas kernels for 0%

profile of v1, /device:TPU:0, one launch (start us, length us, event | category | flops | bytes accessed | tf_op | source)
XLA Modules:
  0.0 827.0 jit_solution(9569353878511323499)
XLA Ops:
  50.3 18.7 %all-reduce.7 = (f32[128]{0:T(128)S(1)}, f32[128]{0:T(128)S(1)}) all-reduce(f32[128]{0:T(128)S(1)} %get-tuple-element.131, f32[128]{0:T(128)S(1)} %get-tuple-element.133), channel_id=1, replica_groups=mesh['dp'=8,'tensor'=4] {'tensor'}, use_global_device_ids=true, to_apply=%region_5.6 | all-reduce | flops 256 | bytes 2048 | tf_op jit(solution)/shard_map/psum | solution.py:140
  101.8 6.9 gather_fusion.2
  108.6 6.6 multiply_convert_fusion
  120.7 67.7 %all-gather = s32[8,1,128]{2,1,0:T(1,128)S(1)} all-gather(s32[1,1,128]{2,1,0:T(1,128)S(1)} %bitcast.186), channel_id=1, replica_groups=mesh['dp'=8,'tensor'=4] {'dp'}, dimensions={0}, use_global_device_ids=true | all-gather | bytes 4608 | tf_op jit(solution)/shard_map/all_gather | solution.py:156
  199.6 35.5 %all-reduce.14.cloned.1.call-done = bf16[128,2048]{1,0:T(8,128)(2,1)} async-done(((bf16[128,2048]{1,0:T(8,128)(2,1)}), bf16[128,2048]{1,0:T(8,128)(2,1)}) %all-reduce.14.cloned.1.call-update) | async-done | bytes 524304 | tf_op jit(solution)/shard_map/psum | solution.py:173
  258.5 49.4 %all-to-all-done = bf16[16,72,2048]{2,1,0:T(8,128)(2,1)} async-done(((bf16[16,72,2048]{2,1,0:T(8,128)(2,1)}), bf16[16,72,2048]{2,1,0:T(8,128)(2,1)}, u32[]{:S(2)}, u32[]{:S(2)}) %all-to-all-start) | async-done | bytes 4718624 | tf_op jit(solution)/shard_map/all_to_all | solution.py:188
  322.7 9.4 %copy.183 = bf16[2,576,2048]{2,0,1:T(2,128)(2,1)} copy(bf16[2,576,2048]{2,1,0:T(8,128)(2,1)} %bitcast_convert_fusion) | data formatting | bytes 9437184 | tf_op jit(solution)/shard_map/convert_element_type | solution.py:211
  337.2 54.2 %all-to-all-done.3 = bf16[2,576,2048]{2,0,1:T(2,128)(2,1)} async-done(((bf16[2,576,2048]{2,0,1:T(2,128)(2,1)}), bf16[2,576,2048]{2,0,1:T(2,128)(2,1)}, u32[]{:S(2)}, u32[]{:S(2)}) %all-to-all-start.3) | async-done | bytes 4718624 | tf_op jit(solution)/shard_map/all_to_all | solution.py:210
  400.8 12.6 %gather_fusion.3 = f32[1024,2048]{1,0:T(8,128)} fusion(f32[1153,2048]{1,0:T(8,128)} %pad_convert_fusion, s32[1024]{0:T(1024)S(1)} %broadcast_clamp_fusion), kind=kCustom, calls=%fused_computation.3 | custom fusion | bytes 16781312 | tf_op jit(solution)/shard_map/gather | solution.py:221
  425.0 9.4 %copy.176 = bf16[2,576,2048]{2,0,1:T(2,128)(2,1)} copy(bf16[2,576,2048]{2,1,0:T(8,128)(2,1)} %convolution_convert_fusion) | data formatting | bytes 9437184 | tf_op jit(solution)/shard_map/convert_element_type | solution.py:208
  439.2 17.1 %all-reduce.16.cloned.1.call-done = bf16[128,2048]{1,0:T(8,128)(2,1)} async-done(((bf16[128,2048]{1,0:T(8,128)(2,1)}), bf16[128,2048]{1,0:T(8,128)(2,1)}) %all-reduce.16.cloned.1.call-update) | async-done | bytes 524304 | tf_op jit(solution)/shard_map/psum | solution.py:224
  464.8 36.2 %all_gather.47 = bf16[1024,4]{0,1:T(4,128)(2,1)S(1)} all-gather(bf16[128,4]{0,1:T(4,128)(2,1)S(1)} %get-tuple-element.113), channel_id=1, replica_groups=mesh['dp'=8,'tensor'=4] {'dp'}, dimensions={0}, use_global_device_ids=true | all-gather | bytes 9216 | tf_op jit(solution)/shard_map/all_gather | solution.py:263
  514.5 12.7 %gather_fusion.1 = f32[1024,2048]{1,0:T(8,128)} fusion(f32[1153,2048]{1,0:T(8,128)} %pad_convert_fusion.1, s32[1024]{0:T(1024)S(1)} %broadcast_clamp_fusion), kind=kCustom, calls=%fused_computation.1 | custom fusion | bytes 16781312 | tf_op jit(solution)/shard_map/gather | solution.py:218
  527.2 7.4 fusion
  534.7 8.2 all_gather.49
  562.7 18.4 %all-reduce.6 = (f32[128]{0:T(128)}, f32[128]{0:T(128)}, bf16[2048]{0:T(1024)(128)(2,1)}, bf16[2048]{0:T(1024)(128)(2,1)}) all-reduce(f32[128]{0:T(128)S(1)} %get-tuple-element.79, f32[128]{0:T(128)S(1)} %get-tuple-element.77, f32[2048]{0:T(1024)S(1)} %dynamic_update_slice.6, ...), channel_id=1, replica_groups=mesh['dp'=8,'tensor'=4] {'tensor'}, use_global_device_ids=true, to_apply=%region_26.27 | all-reduce | flops 4352 | bytes 26624 | tf_op jit(solution)/shard_map/psum | solution.py:300
  605.5 9.5 %convolution_bitcast_fusion = f32[2048,2,2,256]{0,3,2,1:T(8,128)} fusion(bf16[2,576,2048,1]{2,1,3,0:T(8,128)(2,1)} %bitcast.163, bf16[2,576,1,256]{3,1,0,2:T(8,128)(2,1)} %copy-done.54, bf16[2,576,1,256]{3,1,0,2:T(8,128)(2,1)} %copy-done.53), kind=kOutput, calls=%fused_computation.14 | convolution fusion | flops 2416508928 | bytes 14286848 | tf_op jit(solution)/shard_map/ecd,eczf->dezf/dot_general | solution.py:202
  615.0 13.2 %copy.195 = f32[2048,2,2,256]{3,2,1,0:T(2,128)} copy(f32[2048,2,2,256]{0,3,2,1:T(8,128)} %convolution_bitcast_fusion) | data formatting | bytes 16777216
  634.5 7.2 copy.196
  643.2 24.1 %all-reduce.8 = (bf16[2048]{0:T(1024)(128)(2,1)S(1)}, bf16[2048]{0:T(1024)(128)(2,1)S(1)}, bf16[2048]{0:T(1024)(128)(2,1)S(1)}, bf16[2048]{0:T(1024)(128)(2,1)S(1)}) all-reduce(bf16[2048]{0:T(1024)(128)(2,1)S(1)} %get-tuple-element.74, bf16[2048]{0:T(1024)(128)(2,1)S(1)} %copy-done.40, ...), channel_id=6, replica_groups=mesh['dp'=8,'tensor'=4] {'dp'}, use_global_device_ids=true, to_apply=%region_36.37.clone | all-reduce | flops 8192 | bytes 32768
  673.4 11.8 %reduce-scatter.11.cloned.1.call-done = bf16[256,512]{1,0:T(8,128)(2,1)} async-done(((bf16[2048,512]{1,0:T(8,128)(2,1)}), bf16[256,512]{1,0:T(8,128)(2,1)}) %reduce-scatter.11.cloned.1.call-update) | async-done | bytes 262160 | tf_op jit(solution)/shard_map/reduce_scatter | solution.py:337
  687.0 42.6 %reduce-scatter.9.cloned.1.call-done = bf16[256,512]{1,0:T(8,128)(2,1)} async-done(((bf16[2048,512]{1,0:T(8,128)(2,1)}), bf16[256,512]{1,0:T(8,128)(2,1)}) %reduce-scatter.9.cloned.1.call-update) | async-done | bytes 262160 | tf_op jit(solution)/shard_map/reduce_scatter | solution.py:334
  731.4 42.5 %reduce-scatter.7.cloned.1.call-done = bf16[256,512]{1,0:T(8,128)(2,1)} async-done(((bf16[2048,512]{1,0:T(8,128)(2,1)}), bf16[256,512]{1,0:T(8,128)(2,1)}) %reduce-scatter.7.cloned.1.call-update) | async-done | bytes 262160 | tf_op jit(solution)/shard_map/reduce_scatter | solution.py:331
  775.7 42.5 %reduce-scatter.5.cloned.1.call-done = bf16[256,512]{1,0:T(8,128)(2,1)} async-done(((bf16[2048,512]{1,0:T(8,128)(2,1)}), bf16[256,512]{1,0:T(8,128)(2,1)}) %reduce-scatter.5.cloned.1.call-update) | async-done | bytes 262160 | tf_op jit(solution)/shard_map/reduce_scatter | solution.py:328
  (317 shorter events, 247.2 us)
Async XLA Ops:
  7.2 40.8 %all-gather.10.cloned.1.call-start = ((), (), s32[]{:S(2)}) async-start(), calls=%async_computation.8 | async-start | bytes 2359296 | tf_op jit(solution)/shard_map/all_gather | solution.py:132
  7.9 70.3 %all-gather.14.cloned.1.call-start = ((), (), s32[]{:S(2)}) async-start(), calls=%async_computation.10 | async-start | bytes 2359296 | tf_op jit(solution)/shard_map/all_gather | solution.py:134
  8.0 7.9 collective-permute-start
  8.5 17.6 %collective-permute-start.4 = (bf16[256,512]{1,0:T(8,128)(2,1)}, bf16[256,512]{1,0:T(8,128)(2,1)S(1)}, u32[]{:S(2)}, u32[]{:S(2)}) collective-permute-start(bf16[256,512]{1,0:T(8,128)(2,1)} %param.19), channel_id=1, source_target_pairs={{0,28},{4,0},{8,4},{12,8},{16,12},{20,16},{24,20},{28,24},{1,29},{... | collective-permute-start | bytes 786440 | tf_op jit(solution)/shard_map/ppermute | solution.py:22
  11.5 177.4 %all-gather.12.cloned.1.call-start = ((), (), s32[]{:S(2)}) async-start(), calls=%async_computation.9 | async-start | bytes 1179648 | tf_op jit(solution)/shard_map/all_gather | solution.py:154
  26.1 10.6 %collective-permute-start.5 = (bf16[256,512]{1,0:T(8,128)(2,1)S(1)}, bf16[256,512]{1,0:T(8,128)(2,1)}, u32[]{:S(2)}, u32[]{:S(2)}) collective-permute-start(bf16[256,512]{1,0:T(8,128)(2,1)S(1)} %collective-permute-done.4), channel_id=1, source_target_pairs={{0,28},{4,0},{8,4},{12,8},{16,12},{20,16},{24,20},{28,24},{1,29},{... | collective-permute-start | bytes 786440 | tf_op jit(solution)/shard_map/ppermute | solution.py:22
  29.4 9.9 %collective-permute-start.3 = (bf16[256,512]{1,0:T(8,128)(2,1)}, bf16[256,512]{1,0:T(8,128)(2,1)}, u32[]{:S(2)}, u32[]{:S(2)}) collective-permute-start(bf16[256,512]{1,0:T(8,128)(2,1)} %collective-permute-done.2), channel_id=1, source_target_pairs={{0,4},{4,8},{8,12},{12,16},{16,20},{20,24},{24,28},{28,0},{1,5},{5... | collective-permute-start | bytes 786440 | tf_op jit(solution)/shard_map/ppermute | solution.py:20
  36.6 7.6 collective-permute-start.6
  78.2 114.6 %all-gather.16.cloned.1.call-start = ((), (), s32[]{:S(2)}) async-start(), calls=%async_computation.11 | async-start | bytes 1179648 | tf_op jit(solution)/shard_map/all_gather | solution.py:155
  81.2 115.0 %all-gather.18.cloned.1.call-start = ((), (), s32[]{:S(2)}) async-start(), calls=%async_computation.12 | async-start | bytes 2359296 | tf_op jit(solution)/shard_map/all_gather | solution.py:135
  115.2 133.4 %all-to-all-start.2 = ((bf16[16,72,2048]{2,1,0:T(8,128)(2,1)}), bf16[16,72,2048]{2,1,0:T(8,128)(2,1)}, u32[]{:S(2)}, u32[]{:S(2)}) async-start(bf16[16,72,2048]{2,1,0:T(8,128)(2,1)} %multiply_convert_fusion), calls=%async_computation.2 | async-start | bytes 9437184 | tf_op jit(solution)/shard_map/all_to_all | solution.py:189
  120.7 114.5 %all-reduce.14.cloned.1.call-start = ((), (), s32[]{:S(2)}) async-start(), calls=%async_computation.13 | async-start | bytes 1048576 | tf_op jit(solution)/shard_map/psum | solution.py:173
  248.6 59.4 %all-to-all-start = ((bf16[16,72,2048]{2,1,0:T(8,128)(2,1)}), bf16[16,72,2048]{2,1,0:T(8,128)(2,1)}, u32[]{:S(2)}, u32[]{:S(2)}) async-start(bf16[16,72,2048]{2,1,0:T(8,128)(2,1)} %broadcast_multiply_fusion), calls=%async_computation | async-start | bytes 9437184 | tf_op jit(solution)/shard_map/all_to_all | solution.py:188
  332.1 59.3 %all-to-all-start.3 = ((bf16[2,576,2048]{2,0,1:T(2,128)(2,1)}), bf16[2,576,2048]{2,0,1:T(2,128)(2,1)}, u32[]{:S(2)}, u32[]{:S(2)}) async-start(bf16[2,576,2048]{2,0,1:T(2,128)(2,1)} %copy.183), calls=%async_computation.3 | async-start | bytes 9437184 | tf_op jit(solution)/shard_map/all_to_all | solution.py:210
  336.7 119.6 %all-reduce.16.cloned.1.call-start = ((), (), s32[]{:S(2)}) async-start(), calls=%async_computation.14 | async-start | bytes 1048576 | tf_op jit(solution)/shard_map/psum | solution.py:224
  419.6 82.1 %all-gather.20.cloned.1.call-start = ((), (), s32[]{:S(2)}) async-start(), calls=%async_computation.15 | async-start | bytes 1179648 | tf_op jit(solution)/shard_map/all_gather | solution.py:257
  434.4 70.6 %all-to-all-start.1 = ((bf16[2,576,2048]{2,0,1:T(2,128)(2,1)}), bf16[2,576,2048]{2,0,1:T(2,128)(2,1)}, u32[]{:S(2)}, u32[]{:S(2)}) async-start(bf16[2,576,2048]{2,0,1:T(2,128)(2,1)} %copy.176), calls=%async_computation.1 | async-start | bytes 9437184 | tf_op jit(solution)/shard_map/all_to_all | solution.py:207
  439.1 108.6 %all-gather.22.cloned.1.call-start = ((), (), s32[]{:S(2)}) async-start(), calls=%async_computation.16 | async-start | bytes 1179648 | tf_op jit(solution)/shard_map/all_gather | solution.py:260
  463.1 124.5 %all-gather.24.cloned.1.call-start = ((), (), s32[]{:S(2)}) async-start(), calls=%async_computation.17 | async-start | bytes 2359296 | tf_op jit(solution)/shard_map/all_gather | solution.py:229
  463.7 178.0 %all-reduce.18.cloned.1.call-start = ((), (), s32[]{:S(2)}) async-start(), calls=%async_computation.22 | async-start | bytes 2097152 | tf_op jit(solution)/shard_map/psum | solution.py:223
  592.2 93.0 %reduce-scatter.11.cloned.1.call-start = ((), (), s32[]{:S(2)}) async-start(), calls=%async_computation.21 | async-start | bytes 2359296 | tf_op jit(solution)/shard_map/reduce_scatter | solution.py:337
  595.8 133.8 %reduce-scatter.9.cloned.1.call-start = ((), (), s32[]{:S(2)}) async-start(), calls=%async_computation.20 | async-start | bytes 2359296 | tf_op jit(solution)/shard_map/reduce_scatter | solution.py:334
  598.7 175.2 %reduce-scatter.7.cloned.1.call-start = ((), (), s32[]{:S(2)}) async-start(), calls=%async_computation.19 | async-start | bytes 2359296 | tf_op jit(solution)/shard_map/reduce_scatter | solution.py:331
  601.6 216.5 %reduce-scatter.5.cloned.1.call-start = ((), (), s32[]{:S(2)}) async-start(), calls=%async_computation.18 | async-start | bytes 2359296 | tf_op jit(solution)/shard_map/reduce_scatter | solution.py:328
  (59 other events, 1820.8 us)
Sparse Core Ops, SparseCore 0:
  9.9 34.4 all-gather.9
  46.2 30.1 all-gather.13
  78.9 23.3 all-gather.11
  104.6 26.1 all-gather.15
  132.5 55.3 all-gather.17
  199.6 35.4 all-reduce.13
  419.7 36.5 all-reduce.15
  458.2 39.5 all-gather.19
  499.6 22.5 all-gather.21
  523.9 27.7 all-gather.23
  592.3 49.3 all-reduce.17
  644.8 40.3 reduce-scatter.10
  688.4 41.1 reduce-scatter.8
  732.7 41.0 reduce-scatter.6
  777.0 41.1 reduce-scatter.4
